TPU v7x, 128 devices: a whole 4x4x4 slice. The times are simulated.
128 devices in a mesh: gx: 8 (over x, core), gy: 16 (over z, y).
Axes of the slice: x: 4, y: 4, z: 4, core: 2. Of those that a mesh axis runs over, the one named last changes fastest.
Arguments:
- record_keys: int32 [131072], P(('gx', 'gy')), may hold values from 0 to 16777215
- payloads: int32 [131072], P(('gx', 'gy')), may hold values from 0 to 16777215
Outputs:
- sorted_keys: int32 [245760], P(('gx', 'gy'))
- sorted_payloads: int32 [245760], P(('gx', 'gy'))
- bucket_sizes: int32 [128], P(('gx', 'gy'))
- bucket_digest: int32 [128], P(('gx', 'gy'))
All inputs are finite; a program needn't handle non-finite values.
Results may differ from a plain program's by a relative error of at most 0.000001.
Values may be sent and summed in bfloat16 or wider, within the bound.
A program may use at most 64 MiB of HBM per device.

v0:
```python
import jax
import jax.numpy as jnp
from jax import lax
from jax.sharding import PartitionSpec as P

filler = 1073741824


def in_order(blocks, dim):
    dims = list(blocks.shape[1:])
    dims[dim] *= blocks.shape[0]
    return jnp.moveaxis(blocks, 0, dim).reshape(dims)


def gather_packed(arrays, axis, dims):
    line = jnp.concatenate([a.reshape(-1) for a in arrays])
    lines, at, finished = lax.all_gather(line, axis), 0, []
    for a, dim in zip(arrays, dims):
        blocks = lines[:, at : at + a.size].reshape(-1, *a.shape)
        finished.append(in_order(blocks, dim))
        at += a.size
    return tuple(finished)


def beneath_grid(run_keys, run_places, split_keys, split_places):
    return (run_keys[None, :] < split_keys[:, None]) | (
        run_keys[None, :] == split_keys[:, None]
    ) & (run_places[None, :] <= split_places[:, None])


def shards(record_keys, payloads):
    devices = lax.axis_size(("gx", "gy"))
    per_device = record_keys.shape[0]
    spacing = per_device // devices
    bucket_cap = 2 * per_device - devices
    offset = lax.axis_index(("gx", "gy")) * per_device
    places = offset + lax.iota(jnp.int32, per_device)
    run_keys, run_places, run_values = lax.sort((record_keys, places, payloads), num_keys=2)
    sample_keys = run_keys.reshape(devices, spacing)[:, spacing - 1]
    sample_places = run_places.reshape(devices, spacing)[:, spacing - 1]
    every_keys, every_places = gather_packed((sample_keys, sample_places), ("gx", "gy"), (0, 0))
    every_keys, every_places = lax.sort((every_keys, every_places), num_keys=2)
    split_keys = every_keys.reshape(devices, devices)[: devices - 1, devices - 1]
    split_places = every_places.reshape(devices, devices)[: devices - 1, devices - 1]
    beneath = beneath_grid(run_keys, run_places, split_keys, split_places)
    bucket_of = devices - 1 - jnp.sum(beneath.astype(jnp.int32), axis=0)
    owners = lax.iota(jnp.int32, devices)
    mine = bucket_of[None, :] == owners[:, None]
    send_keys = jnp.where(mine, run_keys[None, :], filler)
    send_values = jnp.where(mine, run_values[None, :], filler)
    got_keys, got_values = (
        lax.all_to_all(send_keys, ("gx", "gy"), split_axis=0, concat_axis=0, tiled=True),
        lax.all_to_all(send_values, ("gx", "gy"), split_axis=0, concat_axis=0, tiled=True),
    )
    flat_keys, flat_values = lax.sort(
        (got_keys.reshape(-1), got_values.reshape(-1)), is_stable=True, num_keys=1
    )
    flat_keys = flat_keys[:bucket_cap]
    flat_values = flat_values[:bucket_cap]
    filled = flat_keys < filler
    sorted_keys = jnp.where(filled, flat_keys, -1)
    sorted_payloads = jnp.where(filled, flat_values, -1)
    bucket_size = jnp.sum(filled.astype(jnp.int32)).reshape(1)
    ranks = lax.iota(jnp.int32, bucket_cap)
    mixed = (sorted_keys + 3 * sorted_payloads + 5 * ranks) % 1024
    digest = jnp.sum(jnp.where(filled, 2 * mixed - 1023, 0)).astype(jnp.int32).reshape(1)
    return (sorted_keys, sorted_payloads, bucket_size, digest)


def solution(mesh):
    return jax.shard_map(
        shards,
        mesh=mesh,
        in_specs=(P(("gx", "gy")), P(("gx", "gy"))),
        out_specs=(P(("gx", "gy")), P(("gx", "gy")), P(("gx", "gy")), P(("gx", "gy"))),
        check_vma=False,
    )
```

profile of v0, /device:TPU:0, one launch (start us, length us, event | category | flops | bytes accessed | tf_op | source)
XLA Modules:
  0.0 212.8 jit_solution(15074508309098597869)
XLA Ops:
  7.2 0.0 sort.73.cloned.1.call-start
  7.2 0.0 copy-start
  7.2 0.0 copy-start.1
  7.3 0.6 copy-done
  7.9 0.0 copy-done.1
  7.9 4.5 %sort.69 = (s32[1024]{0:T(1024)S(1)}, s32[1024]{0:T(1024)S(1)}, s32[1024]{0:T(1024)S(1)}, s32[1024]{0:T(1024)}) sort(s32[1024]{0:T(1024)S(1)} %copy-done, s32[1024]{0:T(1024)S(1)} %iota_add_fusion, s32[1024]{0:T(1024)S(1)} %copy-done.1, s32[1024]{0:T(1024)S(1)} %iota.22), dimensions={0}, to_apply=%region_0.0 | sort | flops 10240 | bytes 32768 | tf_op jit(solution)/shard_map/sort | solution.py:38
  12.4 0.1 reshape.138
  12.5 0.1 reshape.137
  12.6 0.2 slice_reduce_fusion.2
  12.8 67.2 %all-gather.1 = s32[128,1,256]{2,1,0:T(1,128)S(1)} all-gather(s32[1,1,256]{2,1,0:T(1,128)S(1)} %bitcast.19), channel_id=2, replica_groups=mesh['gx'=8,'gy'=16] {'gx','gy'}, dimensions={0}, use_global_device_ids=true | all-gather | bytes 132096 | tf_op jit(solution)/shard_map/all_gather | solution.py:17
  80.1 8.5 %sort.70 = (s32[16384]{0:T(1024)S(1)}, s32[16384]{0:T(1024)S(1)}, s32[16384]{0:T(1024)}) sort(s32[16384]{0:T(1024)S(1)} %get-tuple-element.28, s32[16384]{0:T(1024)S(1)} %get-tuple-element.27, s32[16384]{0:T(1024)S(1)} %iota.23), dimensions={0}, to_apply=%region_1.0 | sort | flops 229376 | bytes 393216 | tf_op jit(solution)/shard_map/sort | solution.py:42
  88.5 0.2 slice_reduce_fusion.1
  88.7 0.2 slice_reduce_fusion
  88.9 0.2 convert_reduce_fusion
  89.1 0.7 compare_select_fusion
  89.8 20.2 %all_to_all.12 = s32[128,1,1024]{2,1,0:T(1,128)} all-to-all(s32[128,1,1024]{2,1,0:T(1,128)S(1)} %get-tuple-element.29), channel_id=1, replica_groups=mesh['gx'=8,'gy'=16] {'gx','gy'}, dimensions={0} | all-to-all | bytes 1048576 | tf_op jit(solution)/shard_map/all_to_all | solution.py:53
  110.0 18.2 %all_to_all.13 = s32[128,1,1024]{2,1,0:T(1,128)} all-to-all(s32[128,1,1024]{2,1,0:T(1,128)S(1)} %get-tuple-element.30), channel_id=1, replica_groups=mesh['gx'=8,'gy'=16] {'gx','gy'}, dimensions={0} | all-to-all | bytes 1048576 | tf_op jit(solution)/shard_map/all_to_all | solution.py:52
  128.2 0.0 sort.73.cloned.1.call-update
  128.2 75.7 %sort.73.cloned.1.call-done = (s32[131072]{0:T(1024)}, s32[131072]{0:T(1024)}) async-done(((s32[131072]{0:T(1024)}, s32[131072]{0:T(1024)}), (s32[131072]{0:T(1024)}, s32[131072]{0:T(1024)})) %sort.73.cloned.1.call-update) | async-done | bytes 1048592 | tf_op jit(solution)/shard_map/sort | solution.py:55
  204.0 2.0 fusion.4
  (7 shorter events, 0.0 us)
Async XLA Ops:
  7.2 196.8 %sort.73.cloned.1.call-start = ((), (), s32[]{:S(2)}) async-start(), calls=%async_computation.2 | async-start | bytes 3145760 | tf_op jit(solution)/shard_map/sort | solution.py:55
  7.2 0.7 copy-start
  7.2 0.7 copy-start.1
Sparse Core Ops, SparseCore 0:
  128.4 75.5 sort.75.cloned.1.call-done
  (1 shorter events, 0.0 us)
where the time goes:
time: 217 us; the launch traced here: 213 us
  blocking collectives  106 us (49%)
  local copies, waits for them, and re-layouts  77.2 us (36%)
  other arithmetic  15.8 us (7%)
  between operations  14.1 us (6%)
    sort x2, local copies, waits for them, and re-layouts, shards(): lax.sort((got_keys.reshape(-1), got_values.reshape(-1)), is_stable=True,...  75.8 us
    all_gather x1, blocking collectives, gather_packed(): lines, at, finished = (lax.all_gather(line, axis), 0, [])  67.2 us
    all_to_all x1, blocking collectives, shards(): lax.all_to_all(send_values, ('gx', 'gy'), split_axis=0, concat_axis=0, ti...  20.2 us
    all_to_all x1, blocking collectives, shards(): lax.all_to_all(send_keys, ('gx', 'gy'), split_axis=0, concat_axis=0, tile...  18.2 us
    sort x1, other arithmetic, shards(): every_keys, every_places = lax.sort((every_keys, every_places), num_keys=2)  8.46 us
    sort x1, other arithmetic, shards(): lax.sort((record_keys, places, payloads), num_keys=2)  4.52 us

commit v1 on v0

v1 whole, which is shorter than its diff:
```python
import jax
import jax.numpy as jnp
from jax import lax
from jax.experimental import pallas as pl
from jax.experimental.pallas import tpu as pltpu
from jax.sharding import PartitionSpec as P

filler = 1 << 30
MESH = pl.DeviceIdType.MESH
f32, bf16, i32 = jnp.float32, jnp.bfloat16, jnp.int32


def iota(shape, dim):
    return lax.broadcasted_iota(i32, shape, dim)


def pieces(x):
    return [(x & 255).astype(f32), ((x >> 8) & 255).astype(f32), (x >> 16).astype(f32)]


def joined(p):
    p = [a.astype(i32) for a in p]
    return p[0] + (p[1] << 8) + (p[2] << 16)


def ranks_of(keys, n):
    across = jnp.transpose(keys)
    columns = [
        jnp.broadcast_to(across[:, a : a + 1], (128, 128)).reshape(16, 8, 128) for a in range(n)
    ]
    earlier = (iota((128, 128), 0) < iota((128, 128), 1)).astype(i32).reshape(16, 8, 128)
    ranks = []
    for e in range(n):
        row = keys[e : e + 1, :]
        total = jnp.zeros((8, 128), i32)
        for a in range(n):
            if a < e:
                below = columns[a] <= row
            elif a > e:
                below = columns[a] < row
            else:
                below = columns[a] < row + earlier
            total = total + jnp.sum(below.astype(i32), axis=0)
        ranks.append(jnp.sum(total, axis=0, keepdims=True))
    return ranks


def scattered(ranks, parts, rows):
    left, right = [], []
    high, low = iota((rows, 128), 0), iota((128, 128), 0)
    for rank, part in zip(ranks, parts):
        mine = (rank >> 7) == high
        left.append(
            jnp.concatenate([jnp.where(mine, p, 0.0) for p in part], axis=0).astype(bf16)
        )
        right.append(((rank & 127) == low).astype(f32).astype(bf16))
    left = jnp.concatenate(left, axis=1)
    right = jnp.concatenate(right, axis=1)
    return lax.dot_general(
        left, right, (((1,), (1,)), ((), ())), preferred_element_type=f32
    )


def sort_kernel(keys_ref, values_ref, out_ref):
    keys, values = keys_ref[...], values_ref[...]
    ranks = ranks_of(keys, 8)
    kp, vp = pieces(keys), pieces(values)
    parts = [[p[e : e + 1, :] for p in kp + vp] for e in range(8)]
    got = scattered(ranks, parts, 8)
    out_ref[0:8, :] = joined([got[8 * p : 8 * p + 8] for p in range(3)])
    out_ref[8:16, :] = joined([got[8 * p : 8 * p + 8] for p in range(3, 6)])


def place():
    gx, gy = lax.axis_index("gx"), lax.axis_index("gy")
    return gx, gy


def gather_kernel(run_ref, all_ref, send_sem, recv_sem, pair_send, pair_recv, own_sem):
    gx, gy = place()
    x, core = gx // 2, gx % 2
    z, y = gy // 4, gy % 4
    me = gx * 16 + gy
    own = pltpu.make_async_copy(run_ref, all_ref.at[me], own_sem)
    own.start()
    barrier = pltpu.get_barrier_semaphore()
    xs = [(x + d) % 4 for d in range(4)]
    ys = [(y + d) % 4 for d in range(4)]
    zs = [(z + d) % 4 for d in range(4)]
    peers = []
    for far in (6, 5, 4, 3, 2, 1):
        for dx in range(4):
            for dz in range(4):
                for dy in range(4):
                    if min(dx, 4 - dx) + min(dy, 4 - dy) + min(dz, 4 - dz) == far:
                        peers.append((xs[dx] * 2 + core, zs[dz] * 4 + ys[dy]))
    partner = (x * 2 + 1 - core, gy)
    for p in peers:
        pl.semaphore_signal(barrier, inc=1, device_id=p, device_id_type=MESH)
    pl.semaphore_signal(barrier, inc=1, device_id=partner, device_id_type=MESH)
    pl.semaphore_wait(barrier, 64)
    for p in peers:
        pltpu.make_async_remote_copy(
            src_ref=run_ref, dst_ref=all_ref.at[me], send_sem=send_sem, recv_sem=recv_sem,
            device_id=p, device_id_type=MESH,
        ).start()
    own.wait()
    many = all_ref.at[pl.ds(0, 63)]
    pltpu.make_async_copy(many, many, recv_sem).wait()
    for g in range(4):
        block = all_ref.at[pl.ds((2 * g + core) * 16, 16)]
        pltpu.make_async_remote_copy(
            src_ref=block, dst_ref=block, send_sem=pair_send, recv_sem=pair_recv,
            device_id=partner, device_id_type=MESH,
        ).start()
    half = all_ref.at[pl.ds(0, 64)]
    pltpu.make_async_copy(many, many, send_sem).wait()
    pltpu.make_async_copy(half, half, pair_send).wait()
    pltpu.make_async_copy(half, half, pair_recv).wait()


def merge_kernel(all_ref, keys_ref, values_ref, size_ref, digest_ref, comp_ref):
    gx, gy = place()
    me = gx * 16 + gy

    def chunk(r, c, which):
        return all_ref[pl.ds(128 * r + 8 * which + c, 8, stride=16), :]

    lane = iota((8, 128), 1)
    sample_at = (8 * lane + 7) & 127
    sample_chunk = lane >> 4
    samples = []
    for r in range(16):
        s = jnp.zeros((8, 128), i32)
        for c in range(8):
            v = jnp.take_along_axis(chunk(r, c, 0), sample_at, axis=1)
            s = jnp.where(sample_chunk == c, v, s)
        samples.append(s)
    samples = jnp.concatenate(samples, axis=0)
    samples3 = samples.reshape(16, 8, 128)

    targets = [(me * 128 - 1).astype(f32), (me * 128 + 127).astype(f32)]
    bases = [jnp.zeros((1, 128), i32)] * 2
    for bit in range(21, -1, -3):
        counts = []
        for base in bases:
            rows = []
            for d in range(8):
                least = base + (d << bit)
                c = jnp.sum((samples3 < least).astype(i32), axis=0)
                rows.append(jnp.sum(c, axis=0, keepdims=True))
            counts.append(jnp.concatenate(rows, axis=0).astype(f32))
        for s in range(2):
            total = jnp.broadcast_to(jnp.sum(counts[s], axis=1, keepdims=True), (8, 128))
            fits = (total <= targets[s]).astype(i32)
            digit = jnp.sum(fits, axis=0, keepdims=True) - 1
            bases[s] = bases[s] + (digit << bit)

    ones = jnp.ones((128, 128), bf16)
    lower = (iota((128, 128), 1) < iota((128, 128), 0)).astype(f32).astype(bf16)

    def dot(a, b):
        return jnp.dot(a, b, preferred_element_type=f32)

    def mask16(m):
        return m.astype(f32).astype(bf16)

    bounds = []
    for s in range(2):
        base, target = bases[s], targets[s]
        equal = dot(mask16(samples == base), ones)
        under = dot(mask16(samples < base), ones)
        before = dot(lower, equal.astype(bf16))
        rest = target - jnp.sum(under, axis=0, keepdims=True)
        past = before > rest
        whole = before + equal <= rest
        least = jnp.where(whole, base + 1, base)
        tallies = []
        for r in range(16):
            limit = least[8 * r : 8 * r + 8, :]
            t = jnp.zeros((8, 128), i32)
            for c in range(8):
                t = t + (chunk(r, c, 0) < limit).astype(i32)
            tallies.append(t)
        tally = jnp.concatenate(tallies, axis=0).astype(f32).astype(bf16)
        count = dot(tally, ones)
        cut = 8.0 * (under + rest - before) + 8.0
        bounds.append(jnp.where(past | whole, count, cut).astype(i32))
    begin = jnp.where(me == 0, 0, bounds[0])
    stop = jnp.where(me == 127, 1024, bounds[1])
    length = stop - begin
    coarse = (length >> 3).astype(f32)
    fine = (length & 7).astype(f32)
    offset = (
        8.0 * dot(lower, coarse.astype(bf16)) + dot(lower, fine.astype(bf16))
    ).astype(i32)
    upper = iota((128, 128), 0) < iota((128, 128), 1)
    ones16 = jnp.ones((16, 128), bf16)
    offset_row = (
        8.0 * dot(ones16, jnp.where(upper, coarse, 0.0).astype(bf16))
        + dot(ones16, jnp.where(upper, fine, 0.0).astype(bf16))
    ).astype(i32)
    size = jnp.sum(length, axis=0, keepdims=True)
    longest = jnp.max(length)

    def window(k):
        left = []
        high = iota((16, 128), 0)
        for carry in range(2):
            left.append(mask16((offset_row >> 7) + (k + carry) == high))
        left = jnp.concatenate(left, axis=1)
        first, second = [], []
        for r in range(16):
            b = begin[8 * r : 8 * r + 8, :]
            o = offset[8 * r : 8 * r + 8, :] & 127
            n = length[8 * r : 8 * r + 8, :] - 128 * k
            inner = b & 127
            at = (b >> 7) + k + (lane < inner).astype(i32)
            turn = (inner - o + lane) & 127
            valid = ((lane - o) & 127) < n
            here = valid & (lane >= o)
            over = valid & (lane < o)
            row1, row2 = [], []
            for which in range(2):
                v = chunk(r, 0, which)
                for c in range(1, 8):
                    v = jnp.where(at == c, chunk(r, c, which), v)
                v = jnp.take_along_axis(v, turn, axis=1)
                row1 += pieces(jnp.where(here, v, 0))
                row2 += pieces(jnp.where(over, v, 0))
            first.append(jnp.concatenate(row1, axis=1))
            second.append(jnp.concatenate(row2, axis=1))
        right = jnp.concatenate(first + second, axis=0).astype(bf16)
        return dot(left, right)

    comp_ref[...] = window(0)

    def more(k, _):
        comp_ref[...] += window(k)
        return 0

    lax.fori_loop(1, (longest + 127) >> 7, more, 0)
    comp = comp_ref[...]
    parts = [comp[:, 128 * p : 128 * p + 128] for p in range(6)]
    slot = iota((16, 128), 0) * 128 + iota((16, 128), 1)
    filled = slot < size
    keys = jnp.where(filled, joined(parts[:3]), filler)

    def finish(n):
        ranks = ranks_of(keys, n)
        got = scattered(ranks, [[p[e : e + 1, :] for p in parts] for e in range(n)], 16)
        k = jnp.where(filled, joined([got[16 * p : 16 * p + 16] for p in range(3)]), -1)
        v = jnp.where(filled, joined([got[16 * p : 16 * p + 16] for p in range(3, 6)]), -1)
        keys_ref[...] = k[:15]
        values_ref[...] = v[:15]
        mixed = (k + 3 * v + 5 * slot) & 1023
        digest_ref[0] = jnp.sum(jnp.where(filled, 2 * mixed - 1023, 0))

    total = jnp.max(size)
    size_ref[0] = total

    @pl.when(total <= 1152)
    def _():
        finish(9)

    @pl.when((total > 1152) & (total <= 1280))
    def _():
        finish(10)

    @pl.when(total > 1280)
    def _():
        finish(15)


VM = pl.BlockSpec(memory_space=pltpu.VMEM)
SM = pl.BlockSpec(memory_space=pltpu.SMEM)


def sort_call(keys, values):
    return pl.pallas_call(
        sort_kernel, out_shape=jax.ShapeDtypeStruct((16, 128), i32),
        in_specs=[VM, VM], out_specs=VM, name="sort_block",
    )(keys, values)


def gather_call(run):
    return pl.pallas_call(
        gather_kernel, out_shape=jax.ShapeDtypeStruct((128, 16, 128), i32),
        in_specs=[pl.BlockSpec(memory_space=pl.ANY)], out_specs=VM, name="gather_runs",
        scratch_shapes=[pltpu.SemaphoreType.DMA] * 5,
        compiler_params=pltpu.CompilerParams(collective_id=0, has_side_effects=True),
    )(run)


def merge_call(everything):
    return pl.pallas_call(
        merge_kernel,
        out_shape=(
            jax.ShapeDtypeStruct((15, 128), i32),
            jax.ShapeDtypeStruct((15, 128), i32),
            jax.ShapeDtypeStruct((1,), i32),
            jax.ShapeDtypeStruct((1,), i32),
        ),
        in_specs=[VM], out_specs=(VM, VM, SM, SM), name="merge_bucket",
        scratch_shapes=[pltpu.VMEM((16, 768), f32)],
    )(everything)


def shards(record_keys, payloads):
    run = sort_call(record_keys.reshape(8, 128), payloads.reshape(8, 128))
    everything = gather_call(run)
    k, v, size, digest = merge_call(everything.reshape(2048, 128))
    return k.reshape(1920), v.reshape(1920), size, digest


def solution(mesh):
    spec = P(("gx", "gy"))
    return jax.shard_map(
        shards, mesh=mesh, in_specs=(spec, spec), out_specs=(spec,) * 4, check_vma=False
    )
```

time: 217 us -> 29.7 us (0.14)
  the two profiles are of different devices: /device:TPU:0 before, /device:TPU:1 now
where the time goes in v1:
time: 29.7 us; the launch traced here: 29.5 us
  Pallas kernels  28.9 us (97%)
  between operations  0.64 us (2%)
    pallas_call x1, Pallas kernels, gather_call(): pl.pallas_call(gather_kernel, out_shape=jax.ShapeDtypeStruct((128, 16, 12...  21.1 us
    pallas_call x1, Pallas kernels, merge_call(): pl.pallas_call(merge_kernel, out_shape=(jax.ShapeDtypeStruct((15, 128), i...  5.7 us
    pallas_call x1, Pallas kernels, sort_call(): pl.pallas_call(sort_kernel, out_shape=jax.ShapeDtypeStruct((16, 128), i32...  2.07 us

profile of v1, /device:TPU:1, one launch (start us, length us, event | category | flops | bytes accessed | tf_op | source)
XLA Modules:
  0.0 29.5 jit_solution(4036471148269654320)
XLA Ops:
  0.6 2.1 %sort_block.1.run_ref = s32[16,128]{1,0:T(8,128)} custom-call(s32[8,128]{1,0:T(8,128)} %bitcast.6, s32[8,128]{1,0:T(8,128)} %bitcast.7), custom_call_target="tpu_custom_call" | custom-call | tf_op jit(solution)/shard_map/sort_block/pallas_call | solution.py:280
  2.7 21.1 %gather_runs.1 = s32[128,16,128]{2,1,0:T(8,128)} custom-call(s32[16,128]{1,0:T(8,128)} %sort_block.1.run_ref), custom_call_target="tpu_custom_call" | custom-call | tf_op jit(solution)/shard_map/gather_runs/pallas_call | solution.py:287
  23.8 5.7 %merge_bucket.1 = (s32[15,128]{1,0:T(8,128)}, s32[15,128]{1,0:T(8,128)}, s32[1]{0:T(128)}, s32[1]{0:T(128)}) custom-call(s32[2048,128]{1,0:T(8,128)} %bitcast.5), custom_call_target="tpu_custom_call" | custom-call | tf_op jit(solution)/shard_map/merge_bucket/pallas_call | solution.py:296
